TPU v7x, 32 devices: a whole 2x2x4 slice. The times are simulated.
32 devices in a mesh: group: 4 (over y, x), shard: 8 (over z, core).
Axes of the slice: x: 2, y: 2, z: 4, core: 2. Of those that a mesh axis runs over, the one named last changes fastest.
Arguments:
- grad_pooled: bfloat16 [4096, 512, 128], P(('group', 'shard')), may hold values from -6 to 6
- bag_rows: int32 [4096, 512, 8], P(('group', 'shard')), may hold values from 0 to 511
- bag_lengths: int32 [4096, 512], P(('group', 'shard')), may hold values from 1 to 8
- table_order: int32 [512], replicated, may hold values from 0 to 511, each once
- weights: bfloat16 [512, 512, 128], P('shard'), may hold values from -6 to 6
- accum: float32 [512, 512], P('shard'), may hold values from 0.1 to 10
Outputs:
- new_weights: bfloat16 [512, 512, 128], P('shard')
- new_accum: float32 [512, 512], P('shard')
All inputs are finite; a program needn't handle non-finite values.
Results may differ from a plain program's by a relative error of at most 0.001.
Values may be sent and summed in bfloat16 or wider, within the bound.
A program may use at most 128 MiB of HBM per device.

v0:
```python
import jax
import jax.numpy as jnp
from jax import lax
from jax.sharding import PartitionSpec as P

LEARN_RATE = 0.5
EPSILON = 1e-06


def expand_rows(gradient, row_ids, row_count):
    tables_first = jnp.swapaxes(gradient, 0, 1)
    picks_first = jnp.transpose(row_ids, (1, 2, 0))

    def one_table(member):
        values, chosen = member
        positions = lax.broadcasted_iota(jnp.int32, (row_count, chosen.shape[1]), 0)
        counts = jnp.zeros((row_count, chosen.shape[1]), jnp.float32)
        for column in range(chosen.shape[0]):
            counts = counts + (chosen[column][None, :] == positions).astype(jnp.float32)
        return jnp.dot(counts.astype(jnp.bfloat16), values, preferred_element_type=jnp.float32)

    return lax.map(one_table, (tables_first, picks_first))


def adagrad(weight_rows, accum_rows, row_grad):
    new_accum = accum_rows + jnp.mean(row_grad * row_grad, axis=-1)
    step_size = LEARN_RATE / (jnp.sqrt(new_accum) + EPSILON)
    new_weights = (weight_rows.astype(jnp.float32) - step_size[:, :, None] * row_grad).astype(
        jnp.bfloat16
    )
    return (new_weights, new_accum)


def body(grad_pooled, bag_rows, bag_lengths, table_order, weights, accum):
    row_count = weights.shape[1]
    bag_size = bag_rows.shape[2]
    places = lax.broadcasted_iota(jnp.int32, bag_rows.shape, 2)
    live_rows = jnp.where(places < bag_lengths[:, :, None], bag_rows, -1)
    pooled = jnp.take(grad_pooled, table_order, axis=1)
    chosen = jnp.take(live_rows, table_order, axis=1)
    groups = lax.axis_size("group")
    shards = lax.axis_size("shard")
    quarter = weights.shape[0] // groups
    samples = pooled.shape[0]
    width = pooled.shape[2]
    pooled = pooled.reshape(samples, shards, groups, quarter, width)
    pooled = jnp.transpose(pooled, (0, 2, 1, 3, 4)).reshape(
        samples, shards * groups * quarter, width
    )
    chosen = chosen.reshape(samples, shards, groups, quarter, bag_size)
    chosen = jnp.transpose(chosen, (0, 2, 1, 3, 4)).reshape(
        samples, shards * groups * quarter, bag_size
    )
    gathered = lax.all_to_all(pooled, ("group", "shard"), split_axis=1, concat_axis=0, tiled=True)
    row_ids = lax.all_to_all(chosen, ("group", "shard"), split_axis=1, concat_axis=0, tiled=True)
    row_grad = expand_rows(gathered, row_ids, row_count)
    start = lax.axis_index("group") * quarter
    weight_part = lax.dynamic_slice_in_dim(weights, start, quarter, 0)
    accum_part = lax.dynamic_slice_in_dim(accum, start, quarter, 0)
    part_weights, part_accum = adagrad(weight_part, accum_part, row_grad)
    full_weights, full_accum = (
        lax.all_gather(part_weights.astype(jnp.float32), "group", axis=0, tiled=True),
        lax.all_gather(part_accum, "group", axis=0, tiled=True),
    )
    return (full_weights.astype(jnp.bfloat16), full_accum)


def solution(mesh):
    in_specs = (
        P(("group", "shard"), None, None),
        P(("group", "shard"), None, None),
        P(("group", "shard"), None),
        P(),
        P("shard", None, None),
        P("shard", None),
    )
    out_specs = (P("shard", None, None), P("shard", None))
    return jax.shard_map(body, mesh=mesh, in_specs=in_specs, out_specs=out_specs, check_vma=False)
```

profile of v0, /device:TPU:0, one launch (start us, length us, event | category | flops | bytes accessed | tf_op | source)
XLA Modules:
  0.0 827.4 jit_solution(13259575028350120470)
XLA Ops:
  28.1 55.3 %gather_fusion.1 = bf16[512,128,128]{2,0,1:T(8,128)(2,1)} fusion(bf16[128,512,128]{2,1,0:T(8,128)(2,1)} %param.8, s32[1024]{0:T(1024)S(1)} %pad_clamp_fusion), kind=kCustom, calls=%fused_computation.1 | custom fusion | bytes 33556480 | tf_op jit(solution)/shard_map/jit(_take)/gather | solution.py:39
  83.4 9.1 %copy_select_fusion = bf16[128,8,4,16,128]{4,3,1,2,0:T(8,128)(2,1)S(1)} fusion(bf16[128,8,4,16,128]{4,3,2,1,0:T(8,128)(2,1)} %bitcast.64, pred[8,4,16]{2,0,1:T(8,128)(4,1)S(1)} %copy.25), kind=kLoop, calls=%fused_computation.25 | loop fusion | flops 8388608 | bytes 33554944 | tf_op jit(solution)/shard_map/jit(_take)/select_n | solution.py:39
  92.5 38.2 %copy.27 = bf16[128,512,128]{2,0,1:T(8,128)(2,1)} copy(bf16[128,512,128]{2,1,0:T(8,128)(2,1)S(1)} %bitcast.65) | data formatting | bytes 33554432 | tf_op jit(solution)/shard_map/reshape | solution.py:47
  138.2 362.9 %all-to-all-done.1 = bf16[128,512,128]{2,0,1:T(8,128)(2,1)} async-done(((bf16[128,512,128]{2,0,1:T(8,128)(2,1)}), bf16[128,512,128]{2,0,1:T(8,128)(2,1)}, u32[]{:S(2)}, u32[]{:S(2)}) %all-to-all-start.1) | async-done | bytes 16777248 | tf_op jit(solution)/shard_map/all_to_all | solution.py:54
  501.1 15.2 %copy.29 = bf16[32,128,16,128]{3,2,1,0:T(8,128)(2,1)S(1)} copy(bf16[32,128,16,128]{3,1,2,0:T(8,128)(2,1)} %bitcast.23) | data formatting | bytes 33554432 | tf_op jit(solution)/shard_map/all_to_all | solution.py:54
  516.4 11.9 %copy.30 = bf16[16,4096,128]{2,1,0:T(8,128)(2,1)} copy(bf16[16,4096,128]{2,0,1:T(8,128)(2,1)S(1)} %bitcast.66) | data formatting | bytes 33554432 | tf_op jit(solution)/shard_map/while | solution.py:22
  528.3 190.0 %while.10 = (s32[]{:T(128)}, f32[16,512,128]{2,1,0:T(8,128)}, s32[16,8,4096]{2,1,0:T(8,128)}, bf16[16,4096,128]{2,1,0:T(8,128)(2,1)}, s32[]{:T(128)}, /*index=5*...) while((s32[]{:T(128)}, f32[16,512,128]{2,1,0:T(8,128)}, s32[16,8,4096]{2,1,0:T(8,128)}, ...), condition=%wide.region_1.2_spmd, body=%wide.region_0.1_spmd.sunk | while | flops 587202560 | bytes 1705201 | solution.py:22
  529.9 10.2 %fusion.11 = f32[16,512,128]{2,1,0:T(8,128)} fusion(f32[16,512,128]{2,1,0:T(8,128)} %get-tuple-element.106, s32[]{:T(128)} %get-tuple-element.105, s32[4096]{0:T(1024)S(1)} %bitcast.77, s32[4096]{0:T(1024)S(1)} %bitcast.71, s32[4096]{0:T(1024)S(1)} %bitcast.72, s32[4096]{0:T(1024)S(1)} %bitcast.73, s32[4096]{0:T(1024)S(1)} %bitcast.74, ...), kind=kOutput, calls=%fused_computation.13.clone.1 | convolution fusion | flops 587202560 | bytes 1442816 | tf_op jit(solution)/shard_map/while/body/eval_jaxpr/dot_general | solution.py:20
  541.7 10.2 %fusion.11 = f32[16,512,128]{2,1,0:T(8,128)} fusion(f32[16,512,128]{2,1,0:T(8,128)} %get-tuple-element.106, s32[]{:T(128)} %get-tuple-element.105, s32[4096]{0:T(1024)S(1)} %bitcast.77, s32[4096]{0:T(1024)S(1)} %bitcast.71, s32[4096]{0:T(1024)S(1)} %bitcast.72, s32[4096]{0:T(1024)S(1)} %bitcast.73, s32[4096]{0:T(1024)S(1)} %bitcast.74, ...), kind=kOutput, calls=%fused_computation.13.clone.1 | convolution fusion | flops 587202560 | bytes 1442816 | tf_op jit(solution)/shard_map/while/body/eval_jaxpr/dot_general | solution.py:20
  553.8 10.2 %fusion.11 = f32[16,512,128]{2,1,0:T(8,128)} fusion(f32[16,512,128]{2,1,0:T(8,128)} %get-tuple-element.106, s32[]{:T(128)} %get-tuple-element.105, s32[4096]{0:T(1024)S(1)} %bitcast.77, s32[4096]{0:T(1024)S(1)} %bitcast.71, s32[4096]{0:T(1024)S(1)} %bitcast.72, s32[4096]{0:T(1024)S(1)} %bitcast.73, s32[4096]{0:T(1024)S(1)} %bitcast.74, ...), kind=kOutput, calls=%fused_computation.13.clone.1 | convolution fusion | flops 587202560 | bytes 1442816 | tf_op jit(solution)/shard_map/while/body/eval_jaxpr/dot_general | solution.py:20
  565.6 10.2 %fusion.11 = f32[16,512,128]{2,1,0:T(8,128)} fusion(f32[16,512,128]{2,1,0:T(8,128)} %get-tuple-element.106, s32[]{:T(128)} %get-tuple-element.105, s32[4096]{0:T(1024)S(1)} %bitcast.77, s32[4096]{0:T(1024)S(1)} %bitcast.71, s32[4096]{0:T(1024)S(1)} %bitcast.72, s32[4096]{0:T(1024)S(1)} %bitcast.73, s32[4096]{0:T(1024)S(1)} %bitcast.74, ...), kind=kOutput, calls=%fused_computation.13.clone.1 | convolution fusion | flops 587202560 | bytes 1442816 | tf_op jit(solution)/shard_map/while/body/eval_jaxpr/dot_general | solution.py:20
  577.4 10.2 %fusion.11 = f32[16,512,128]{2,1,0:T(8,128)} fusion(f32[16,512,128]{2,1,0:T(8,128)} %get-tuple-element.106, s32[]{:T(128)} %get-tuple-element.105, s32[4096]{0:T(1024)S(1)} %bitcast.77, s32[4096]{0:T(1024)S(1)} %bitcast.71, s32[4096]{0:T(1024)S(1)} %bitcast.72, s32[4096]{0:T(1024)S(1)} %bitcast.73, s32[4096]{0:T(1024)S(1)} %bitcast.74, ...), kind=kOutput, calls=%fused_computation.13.clone.1 | convolution fusion | flops 587202560 | bytes 1442816 | tf_op jit(solution)/shard_map/while/body/eval_jaxpr/dot_general | solution.py:20
  589.5 10.2 %fusion.11 = f32[16,512,128]{2,1,0:T(8,128)} fusion(f32[16,512,128]{2,1,0:T(8,128)} %get-tuple-element.106, s32[]{:T(128)} %get-tuple-element.105, s32[4096]{0:T(1024)S(1)} %bitcast.77, s32[4096]{0:T(1024)S(1)} %bitcast.71, s32[4096]{0:T(1024)S(1)} %bitcast.72, s32[4096]{0:T(1024)S(1)} %bitcast.73, s32[4096]{0:T(1024)S(1)} %bitcast.74, ...), kind=kOutput, calls=%fused_computation.13.clone.1 | convolution fusion | flops 587202560 | bytes 1442816 | tf_op jit(solution)/shard_map/while/body/eval_jaxpr/dot_general | solution.py:20
  601.3 10.2 %fusion.11 = f32[16,512,128]{2,1,0:T(8,128)} fusion(f32[16,512,128]{2,1,0:T(8,128)} %get-tuple-element.106, s32[]{:T(128)} %get-tuple-element.105, s32[4096]{0:T(1024)S(1)} %bitcast.77, s32[4096]{0:T(1024)S(1)} %bitcast.71, s32[4096]{0:T(1024)S(1)} %bitcast.72, s32[4096]{0:T(1024)S(1)} %bitcast.73, s32[4096]{0:T(1024)S(1)} %bitcast.74, ...), kind=kOutput, calls=%fused_computation.13.clone.1 | convolution fusion | flops 587202560 | bytes 1442816 | tf_op jit(solution)/shard_map/while/body/eval_jaxpr/dot_general | solution.py:20
  613.1 10.2 %fusion.11 = f32[16,512,128]{2,1,0:T(8,128)} fusion(f32[16,512,128]{2,1,0:T(8,128)} %get-tuple-element.106, s32[]{:T(128)} %get-tuple-element.105, s32[4096]{0:T(1024)S(1)} %bitcast.77, s32[4096]{0:T(1024)S(1)} %bitcast.71, s32[4096]{0:T(1024)S(1)} %bitcast.72, s32[4096]{0:T(1024)S(1)} %bitcast.73, s32[4096]{0:T(1024)S(1)} %bitcast.74, ...), kind=kOutput, calls=%fused_computation.13.clone.1 | convolution fusion | flops 587202560 | bytes 1442816 | tf_op jit(solution)/shard_map/while/body/eval_jaxpr/dot_general | solution.py:20
  625.1 10.2 %fusion.11 = f32[16,512,128]{2,1,0:T(8,128)} fusion(f32[16,512,128]{2,1,0:T(8,128)} %get-tuple-element.106, s32[]{:T(128)} %get-tuple-element.105, s32[4096]{0:T(1024)S(1)} %bitcast.77, s32[4096]{0:T(1024)S(1)} %bitcast.71, s32[4096]{0:T(1024)S(1)} %bitcast.72, s32[4096]{0:T(1024)S(1)} %bitcast.73, s32[4096]{0:T(1024)S(1)} %bitcast.74, ...), kind=kOutput, calls=%fused_computation.13.clone.1 | convolution fusion | flops 587202560 | bytes 1442816 | tf_op jit(solution)/shard_map/while/body/eval_jaxpr/dot_general | solution.py:20
  636.9 10.2 %fusion.11 = f32[16,512,128]{2,1,0:T(8,128)} fusion(f32[16,512,128]{2,1,0:T(8,128)} %get-tuple-element.106, s32[]{:T(128)} %get-tuple-element.105, s32[4096]{0:T(1024)S(1)} %bitcast.77, s32[4096]{0:T(1024)S(1)} %bitcast.71, s32[4096]{0:T(1024)S(1)} %bitcast.72, s32[4096]{0:T(1024)S(1)} %bitcast.73, s32[4096]{0:T(1024)S(1)} %bitcast.74, ...), kind=kOutput, calls=%fused_computation.13.clone.1 | convolution fusion | flops 587202560 | bytes 1442816 | tf_op jit(solution)/shard_map/while/body/eval_jaxpr/dot_general | solution.py:20
  648.7 10.2 %fusion.11 = f32[16,512,128]{2,1,0:T(8,128)} fusion(f32[16,512,128]{2,1,0:T(8,128)} %get-tuple-element.106, s32[]{:T(128)} %get-tuple-element.105, s32[4096]{0:T(1024)S(1)} %bitcast.77, s32[4096]{0:T(1024)S(1)} %bitcast.71, s32[4096]{0:T(1024)S(1)} %bitcast.72, s32[4096]{0:T(1024)S(1)} %bitcast.73, s32[4096]{0:T(1024)S(1)} %bitcast.74, ...), kind=kOutput, calls=%fused_computation.13.clone.1 | convolution fusion | flops 587202560 | bytes 1442816 | tf_op jit(solution)/shard_map/while/body/eval_jaxpr/dot_general | solution.py:20
  660.6 10.2 %fusion.11 = f32[16,512,128]{2,1,0:T(8,128)} fusion(f32[16,512,128]{2,1,0:T(8,128)} %get-tuple-element.106, s32[]{:T(128)} %get-tuple-element.105, s32[4096]{0:T(1024)S(1)} %bitcast.77, s32[4096]{0:T(1024)S(1)} %bitcast.71, s32[4096]{0:T(1024)S(1)} %bitcast.72, s32[4096]{0:T(1024)S(1)} %bitcast.73, s32[4096]{0:T(1024)S(1)} %bitcast.74, ...), kind=kOutput, calls=%fused_computation.13.clone.1 | convolution fusion | flops 587202560 | bytes 1442816 | tf_op jit(solution)/shard_map/while/body/eval_jaxpr/dot_general | solution.py:20
  672.4 10.2 %fusion.11 = f32[16,512,128]{2,1,0:T(8,128)} fusion(f32[16,512,128]{2,1,0:T(8,128)} %get-tuple-element.106, s32[]{:T(128)} %get-tuple-element.105, s32[4096]{0:T(1024)S(1)} %bitcast.77, s32[4096]{0:T(1024)S(1)} %bitcast.71, s32[4096]{0:T(1024)S(1)} %bitcast.72, s32[4096]{0:T(1024)S(1)} %bitcast.73, s32[4096]{0:T(1024)S(1)} %bitcast.74, ...), kind=kOutput, calls=%fused_computation.13.clone.1 | convolution fusion | flops 587202560 | bytes 1442816 | tf_op jit(solution)/shard_map/while/body/eval_jaxpr/dot_general | solution.py:20
  684.2 10.2 %fusion.11 = f32[16,512,128]{2,1,0:T(8,128)} fusion(f32[16,512,128]{2,1,0:T(8,128)} %get-tuple-element.106, s32[]{:T(128)} %get-tuple-element.105, s32[4096]{0:T(1024)S(1)} %bitcast.77, s32[4096]{0:T(1024)S(1)} %bitcast.71, s32[4096]{0:T(1024)S(1)} %bitcast.72, s32[4096]{0:T(1024)S(1)} %bitcast.73, s32[4096]{0:T(1024)S(1)} %bitcast.74, ...), kind=kOutput, calls=%fused_computation.13.clone.1 | convolution fusion | flops 587202560 | bytes 1442816 | tf_op jit(solution)/shard_map/while/body/eval_jaxpr/dot_general | solution.py:20
  696.3 10.2 %fusion.11 = f32[16,512,128]{2,1,0:T(8,128)} fusion(f32[16,512,128]{2,1,0:T(8,128)} %get-tuple-element.106, s32[]{:T(128)} %get-tuple-element.105, s32[4096]{0:T(1024)S(1)} %bitcast.77, s32[4096]{0:T(1024)S(1)} %bitcast.71, s32[4096]{0:T(1024)S(1)} %bitcast.72, s32[4096]{0:T(1024)S(1)} %bitcast.73, s32[4096]{0:T(1024)S(1)} %bitcast.74, ...), kind=kOutput, calls=%fused_computation.13.clone.1 | convolution fusion | flops 587202560 | bytes 1442816 | tf_op jit(solution)/shard_map/while/body/eval_jaxpr/dot_general | solution.py:20
  708.1 10.2 %fusion.11 = f32[16,512,128]{2,1,0:T(8,128)} fusion(f32[16,512,128]{2,1,0:T(8,128)} %get-tuple-element.106, s32[]{:T(128)} %get-tuple-element.105, s32[4096]{0:T(1024)S(1)} %bitcast.77, s32[4096]{0:T(1024)S(1)} %bitcast.71, s32[4096]{0:T(1024)S(1)} %bitcast.72, s32[4096]{0:T(1024)S(1)} %bitcast.73, s32[4096]{0:T(1024)S(1)} %bitcast.74, ...), kind=kOutput, calls=%fused_computation.13.clone.1 | convolution fusion | flops 587202560 | bytes 1442816 | tf_op jit(solution)/shard_map/while/body/eval_jaxpr/dot_general | solution.py:20
  734.3 77.8 %all-gather.2.cloned.1.call-done = bf16[64,512,128]{2,1,0:T(8,128)(2,1)} async-done(((bf16[16,512,128]{2,1,0:T(8,128)(2,1)}), bf16[64,512,128]{2,1,0:T(8,128)(2,1)}) %all-gather.2.cloned.1.call-update) | async-done | bytes 8388624 | tf_op jit(solution)/shard_map/all_gather | solution.py:62
  (40 shorter events, 79.7 us)
Async XLA Ops:
  20.7 109.9 %all-to-all-start = ((s32[128,512,8]{0,2,1:T(8,128)}), s32[128,512,8]{0,2,1:T(8,128)S(1)}, u32[]{:S(2)}, u32[]{:S(2)}) async-start(s32[128,512,8]{0,2,1:T(8,128)} %bitcast.68), calls=%async_computation | async-start | bytes 4194304 | tf_op jit(solution)/shard_map/all_to_all | solution.py:55
  130.6 370.5 %all-to-all-start.1 = ((bf16[128,512,128]{2,0,1:T(8,128)(2,1)}), bf16[128,512,128]{2,0,1:T(8,128)(2,1)}, u32[]{:S(2)}, u32[]{:S(2)}) async-start(bf16[128,512,128]{2,0,1:T(8,128)(2,1)} %copy.27), calls=%async_computation.1 | async-start | bytes 33554432 | tf_op jit(solution)/shard_map/all_to_all | solution.py:54
  136.6 675.5 %all-gather.2.cloned.1.call-start = ((), (), s32[]{:S(2)}) async-start(), calls=%async_computation.2 | async-start | bytes 10485760 | tf_op jit(solution)/shard_map/all_gather | solution.py:62
Sparse Core Ops, SparseCore 0:
  727.0 85.1 all-gather.1
where the time goes:
time: 829 us; the launch traced here: 827 us
  waiting for transfers between devices  441 us (53%)
  local copies, waits for them, and re-layouts  166 us (20%)
  matrix products  163 us (20%)
  other arithmetic  22.7 us (3%)
  between operations  14.1 us (2%)
  starting transfers between devices  13.3 us (2%)
    all_to_all x1, waiting for transfers between devices, body(): lax.all_to_all(pooled, ('group', 'shard'), split_axis=1, concat_axis=0, t...  363 us
    dot_general x16, matrix products, one_table(): jnp.dot(counts.astype(jnp.bfloat16), values, preferred_element_type=jnp.f...  163 us
    all_gather x1, waiting for transfers between devices, body(): lax.all_gather(part_weights.astype(jnp.float32), 'group', axis=0, tiled=T...  77.8 us
    gather x1, local copies, waits for them, and re-layouts, body(): pooled = jnp.take(grad_pooled, table_order, axis=1)  55.3 us
    reshape x1, local copies, waits for them, and re-layouts, body(): jnp.transpose(pooled, (0, 2, 1, 3, 4))  38.2 us
    slice x16, local copies, waits for them, and re-layouts, one_table(): counts = counts + (chosen[column][None, :] == positions).astype(jnp.float32)  26.8 us
  transfers between devices with their start and end apart: 3, of which 2 were waited for; matrix products, arithmetic and copies ran while one was open for 13% of the time, Pallas kernels for 0%

commit v1 on v0

v1 whole, which is shorter than its diff:
```python
import functools

import jax
import jax.numpy as jnp
from jax import lax
from jax.experimental import pallas as pl
from jax.experimental.pallas import tpu as pltpu
from jax.sharding import PartitionSpec as P

LEARN_RATE = 0.5
EPSILON = 1e-06
AXES = ("group", "shard")
CHUNKS = 4
TILE = 16


def arrange_kernel(order_ref, grad_ref, *rest):
    *outs, flipped = rest
    tables = grad_ref.shape[1]
    part = outs[0].shape[0]

    def flip(step, carry):
        start = pl.multiple_of(step * TILE, TILE)
        block = grad_ref[:, pl.ds(start, TILE), :]
        flipped[pl.ds(start, TILE)] = jnp.swapaxes(block, 0, 1)
        return carry

    lax.fori_loop(0, tables // TILE, flip, 0)
    for chunk, out in enumerate(outs):

        def place(step, carry, chunk=chunk, out=out):
            for k in range(8):
                at = step * 8 + k
                out[at] = flipped[order_ref[chunk * part + at]]
            return carry

        lax.fori_loop(0, part // 8, place, 0)


def arrange(grad_pooled, order, chunks):
    samples, tables, width = grad_pooled.shape
    part = tables // chunks
    return pl.pallas_call(
        arrange_kernel,
        grid_spec=pltpu.PrefetchScalarGridSpec(
            num_scalar_prefetch=1,
            grid=(samples // TILE,),
            in_specs=[pl.BlockSpec((TILE, tables, width), lambda b, order: (b, 0, 0))],
            out_specs=[
                pl.BlockSpec((part, TILE, width), lambda b, order: (0, b, 0))
                for _ in range(chunks)
            ],
            scratch_shapes=[pltpu.VMEM((tables, TILE, width), grad_pooled.dtype)],
        ),
        out_shape=[
            jax.ShapeDtypeStruct((part, samples, width), grad_pooled.dtype)
            for _ in range(chunks)
        ],
        cost_estimate=pl.CostEstimate(
            flops=0, bytes_accessed=4 * grad_pooled.size, transcendentals=0
        ),
    )(order, grad_pooled)


def expand_kernel(offset, unroll, rows_ref, grad_ref, out_ref, counts):
    sources, _, bag, samples = rows_ref.shape
    row_count = out_ref.shape[1]
    place = lax.broadcasted_iota(jnp.int32, (TILE, samples), 0).astype(jnp.float32)
    places = [(place + float(r * TILE - offset)).astype(jnp.bfloat16) for r in range(row_count // TILE)]
    one = jnp.ones((TILE, samples), jnp.bfloat16)
    zero = jnp.zeros((TILE, samples), jnp.bfloat16)
    out_ref[...] = jnp.zeros_like(out_ref)

    def step(i, carry):
        for u in range(unroll):
            picks = rows_ref[i * unroll + u, 0].astype(jnp.float32)
            spread = [
                jnp.broadcast_to(picks[j : j + 1], (TILE, samples)).astype(jnp.bfloat16)
                for j in range(bag)
            ]
            for r, here in enumerate(places):
                terms = [jnp.where(s == here, one, zero) for s in spread]
                while len(terms) > 1:
                    terms = [a + b for a, b in zip(terms[::2], terms[1::2])] + (
                        [terms[-1]] if len(terms) % 2 else []
                    )
                counts[r * TILE : (r + 1) * TILE, u * samples : (u + 1) * samples] = terms[0]
        values = grad_ref[pl.ds(i * unroll, unroll), 0].reshape(unroll * samples, -1)
        out_ref[0] += jnp.dot(counts[...], values, preferred_element_type=jnp.float32)
        return carry

    lax.fori_loop(0, sources // unroll, step, 0)


def expand_rows(gradient, row_ids, first, row_count, offset):
    sources, tables, samples, width = gradient.shape
    bag = row_ids.shape[2]
    unroll = 4 if sources % 4 == 0 else 1
    return pl.pallas_call(
        functools.partial(expand_kernel, offset, unroll),
        grid=(tables,),
        in_specs=[
            pl.BlockSpec((sources, 1, bag, samples), lambda t: (0, first + t, 0, 0)),
            pl.BlockSpec((sources, 1, samples, width), lambda t: (0, t, 0, 0)),
        ],
        out_specs=pl.BlockSpec((1, row_count, width), lambda t: (t, 0, 0)),
        out_shape=jax.ShapeDtypeStruct((tables, row_count, width), jnp.float32),
        scratch_shapes=[pltpu.VMEM((row_count, unroll * samples), jnp.bfloat16)],
        cost_estimate=pl.CostEstimate(
            flops=40 * gradient.size * row_count // 8,
            bytes_accessed=2 * gradient.size,
            transcendentals=0,
        ),
    )(row_ids, gradient)


def body(grad_pooled, bag_rows, bag_lengths, table_order, weights, accum):
    row_count = weights.shape[1]
    samples, tables, width = grad_pooled.shape
    bag = bag_rows.shape[2]
    groups = lax.axis_size("group")
    shards = lax.axis_size("shard")
    devices = groups * shards
    held = weights.shape[0]
    quarter = held // groups
    chunks = CHUNKS if quarter % CHUNKS == 0 else 1
    each = quarter // chunks
    offset = row_count // 2
    me = lax.axis_index("group")

    by_slot = table_order.reshape(shards, chunks, groups, each)
    by_chunk = by_slot.transpose(1, 2, 0, 3).reshape(-1)
    by_device = by_slot.transpose(2, 0, 1, 3).reshape(-1)

    live = jnp.arange(bag, dtype=jnp.int32)[None, :, None] < bag_lengths[:, None, :]
    ids = jnp.where(live, jnp.transpose(bag_rows, (0, 2, 1)), row_count) - offset
    ids = jnp.transpose(ids.astype(jnp.float32), (2, 1, 0))
    ids = jnp.take(ids, by_device, axis=0, mode="clip", unique_indices=True).astype(jnp.bfloat16)
    ids = lax.all_to_all(ids, AXES, split_axis=0, concat_axis=0, tiled=True)
    ids = ids.reshape(devices, quarter, bag, samples)

    sends = arrange(grad_pooled, by_chunk, chunks)
    received = []
    for chunk in range(chunks):
        send = sends[chunk]
        if received:
            send, received[-1] = lax.optimization_barrier((send, received[-1]))
        received.append(lax.all_to_all(send, AXES, split_axis=0, concat_axis=0, tiled=True))

    weights_by = weights.reshape(chunks, groups, each, row_count, width)
    accum_by = accum.reshape(chunks, groups, each, row_count)
    full_weights, sums = [], []
    for chunk in range(chunks):
        gradient = received[chunk].reshape(devices, each, samples, width)
        row_grad = expand_rows(gradient, ids, chunk * each, row_count, offset)
        weight_part = lax.dynamic_index_in_dim(weights_by[chunk], me, 0, keepdims=False)
        accum_part = lax.dynamic_index_in_dim(accum_by[chunk], me, 0, keepdims=False)
        new_accum = accum_part + jnp.mean(row_grad * row_grad, axis=-1)
        step_size = LEARN_RATE / (jnp.sqrt(new_accum) + EPSILON)
        new_weights = weight_part.astype(jnp.float32) - step_size[:, :, None] * row_grad
        full_weights.append(
            lax.all_gather(new_weights.astype(jnp.bfloat16), "group", axis=0, tiled=True)
        )
        sums.append(new_accum)
    all_sums = lax.all_gather(jnp.stack(sums), "group", axis=1)
    return (
        jnp.concatenate(full_weights, axis=0),
        all_sums.reshape(held, row_count),
    )


def solution(mesh):
    in_specs = (
        P(AXES, None, None),
        P(AXES, None, None),
        P(AXES, None),
        P(),
        P("shard", None, None),
        P("shard", None),
    )
    out_specs = (P("shard", None, None), P("shard", None))
    return jax.shard_map(body, mesh=mesh, in_specs=in_specs, out_specs=out_specs, check_vma=False)
```

time: 829 us -> 534 us (0.64)
  waiting for transfers between devices: 441 us -> 241 us
  matrix products: 163 us -> 0 us
  local copies, waits for them, and re-layouts: 166 us -> 14.1 us
  Pallas kernels: 0 us -> 116 us
  blocking collectives: 7.48 us -> 110 us
    dot_general x16 -> x0, matrix products: 163 us -> none  [one_table(): jnp.dot(counts.astype(jnp.bfloat16), values, preferred_element_type=jnp.f...]
    all_to_all x2 -> x4, waiting for transfers between devices: 363 us -> 217 us  [the longest x3 189 us: body(): lax.all_to_all(send, AXES, split_axis=0, concat_axis=0, tiled=True)]
    pallas_call x0 -> x5, Pallas kernels: none -> 116 us  [the longest x4 95.6 us: expand_rows(): pl.pallas_call(functools.partial(expand_kernel, offset, unroll), grid=(ta...]
    all_to_all x0 -> x1, blocking collectives: none -> 102 us  [body(): lax.all_to_all(send, AXES, split_axis=0, concat_axis=0, tiled=True)]
    gather x2 -> x1, local copies, waits for them, and re-layouts: 58 us -> 2.37 us  [body(): jnp.take(ids, by_device, axis=0, mode='clip', unique_indices=True)]
    all_gather x1 -> x4, waiting for transfers between devices: 77.8 us -> 24.4 us  [body(): lax.all_gather(new_weights.astype(jnp.bfloat16), 'group', axis=0, tiled=T...]
    reshape x1 -> x2, local copies, waits for them, and re-layouts: 38.2 us -> 1.5 us  [the longest x1 0.81 us: body(): by_slot = table_order.reshape(shards, chunks, groups, each)]
    slice x16 -> x2, local copies, waits for them, and re-layouts: 26.8 us -> 5.73 us  [the longest x1 5.72 us: body(): weights_by[chunk]]
  transfers between devices with their start and end apart: 3 -> 8, of which waited for: 2 -> 5; matrix products, arithmetic and copies ran while one was open for 13% -> 5% of each run, Pallas kernels for 0% -> 18%
where the time goes in v1:
time: 534 us; the launch traced here: 533 us
  waiting for transfers between devices  241 us (45%)
  Pallas kernels  116 us (22%)
  blocking collectives  110 us (21%)
  other arithmetic  23.9 us (4%)
  local copies, waits for them, and re-layouts  14.1 us (3%)
  between operations  14 us (3%)
  starting transfers between devices  13.6 us (3%)
    all_to_all x3, waiting for transfers between devices, body(): lax.all_to_all(send, AXES, split_axis=0, concat_axis=0, tiled=True)  189 us
    all_to_all x1, blocking collectives, body(): lax.all_to_all(send, AXES, split_axis=0, concat_axis=0, tiled=True)  102 us
    pallas_call x4, Pallas kernels, expand_rows(): pl.pallas_call(functools.partial(expand_kernel, offset, unroll), grid=(ta...  95.6 us
    all_to_all x1, waiting for transfers between devices, body(): ids = lax.all_to_all(ids, AXES, split_axis=0, concat_axis=0, tiled=True)  27.5 us
    all_gather x4, waiting for transfers between devices, body(): lax.all_gather(new_weights.astype(jnp.bfloat16), 'group', axis=0, tiled=T...  24.4 us
    pallas_call x1, Pallas kernels, arrange(): pl.pallas_call(arrange_kernel, grid_spec=pltpu.PrefetchScalarGridSpec(num...  20.4 us
    all_to_all x3, starting transfers between devices, body(): lax.all_to_all(send, AXES, split_axis=0, concat_axis=0, tiled=True)  10.7 us
  transfers between devices with their start and end apart: 8, of which 5 were waited for; matrix products, arithmetic and copies ran while one was open for 5% of the time, Pallas kernels for 18%

profile of v1, /device:TPU:0, one launch (start us, length us, event | category | flops | bytes accessed | tf_op | source)
XLA Modules:
  0.0 532.7 jit_solution(918405155562617016)
XLA Ops:
  8.7 20.4 %shard_map.77 = (bf16[128,128,128]{2,1,0:T(8,128)(2,1)}, bf16[128,128,128]{2,1,0:T(8,128)(2,1)}, bf16[128,128,128]{2,1,0:T(8,128)(2,1)}, bf16[128,128,128]{2,1,0:T(8,128)(2,1)}) custom-call(s32[512]{0:T(512)} %reshape.139.order_ref, bf16[128,512,128]{2,1,0:T(8,128)(2,1)} %grad_ref.1), custom_call_target="tpu_custom_call" | custom-call | bytes 33554432 | tf_op jit(solution)/shard_map/pallas_call | solution.py:43
  29.1 102.3 %all_to_all.25 = bf16[128,128,128]{2,1,0:T(8,128)(2,1)} all-to-all(bf16[128,128,128]{2,1,0:T(8,128)(2,1)} %get-tuple-element.13), channel_id=1, replica_groups=mesh['group'=4,'shard'=8] {'group','shard'}, dimensions={0} | all-to-all | bytes 8388608 | tf_op jit(solution)/shard_map/all_to_all | solution.py:148
  131.4 3.6 all-to-all-start.2
  135.2 2.3 copy.21
  138.0 2.4 gather_fusion
  140.4 89.6 %all-to-all-done.2 = bf16[128,128,128]{2,1,0:T(8,128)(2,1)} async-done(((bf16[128,128,128]{2,1,0:T(8,128)(2,1)}), bf16[128,128,128]{2,1,0:T(8,128)(2,1)}, u32[]{:S(2)}, u32[]{:S(2)}) %all-to-all-start.2) | async-done | bytes 4194336 | tf_op jit(solution)/shard_map/all_to_all | solution.py:148
  230.0 2.6 all-to-all-start
  232.6 27.5 %all-to-all-done = bf16[512,8,128]{2,1,0:T(8,128)(2,1)S(1)} async-done(((bf16[512,8,128]{2,1,0:T(8,128)(2,1)}), bf16[512,8,128]{2,1,0:T(8,128)(2,1)S(1)}, u32[]{:S(2)}, u32[]{:S(2)}) %all-to-all-start) | async-done | bytes 1048608 | tf_op jit(solution)/shard_map/all_to_all | solution.py:139
  261.2 3.6 all-to-all-start.3
  264.9 5.7 %fusion.18 = (bf16[16,512,128]{2,1,0:T(8,128)(2,1)}, bf16[16,512,128]{2,1,0:T(8,128)(2,1)}, bf16[16,512,128]{2,1,0:T(8,128)(2,1)S(1)}, bf16[16,512,128]{2,1,0:T(8,128)(2,1)}) fusion(bf16[64,512,128]{2,1,0:T(8,128)(2,1)} %param.10), kind=kLoop, calls=%fused_computation.40 | loop fusion | bytes 16777216 | tf_op jit(solution)/shard_map/slice | solution.py:156
  270.6 23.9 %shard_map.78 = f32[4,512,128]{2,1,0:T(8,128)} custom-call(bf16[32,16,8,128]{3,2,1,0:T(8,128)(2,1)} %bitcast.78, bf16[32,4,128,128]{3,2,1,0:T(8,128)(2,1)} %bitcast.73), custom_call_target="tpu_custom_call" | custom-call | flops 5368709120 | bytes 4194304 | tf_op jit(solution)/shard_map/pallas_call | solution.py:99
  296.1 2.5 fusion.5
  298.6 61.1 %all-to-all-done.3 = bf16[128,128,128]{2,1,0:T(8,128)(2,1)} async-done(((bf16[128,128,128]{2,1,0:T(8,128)(2,1)}), bf16[128,128,128]{2,1,0:T(8,128)(2,1)}, u32[]{:S(2)}, u32[]{:S(2)}) %all-to-all-start.3) | async-done | bytes 4194336 | tf_op jit(solution)/shard_map/all_to_all | solution.py:148
  359.7 3.6 all-to-all-start.4
  363.3 23.9 %shard_map.79 = f32[4,512,128]{2,1,0:T(8,128)} custom-call(bf16[32,16,8,128]{3,2,1,0:T(8,128)(2,1)} %bitcast.79, bf16[32,4,128,128]{3,2,1,0:T(8,128)(2,1)} %bitcast.12.grad_ref), custom_call_target="tpu_custom_call" | custom-call | flops 5368709120 | bytes 4194304 | tf_op jit(solution)/shard_map/pallas_call | solution.py:99
  388.9 2.5 fusion.4
  391.5 23.9 %shard_map.80 = f32[4,512,128]{2,1,0:T(8,128)} custom-call(bf16[32,16,8,128]{3,2,1,0:T(8,128)(2,1)} %bitcast.80, bf16[32,4,128,128]{3,2,1,0:T(8,128)(2,1)} %bitcast.16.grad_ref), custom_call_target="tpu_custom_call" | custom-call | flops 5368709120 | bytes 4194304 | tf_op jit(solution)/shard_map/pallas_call | solution.py:99
  417.0 2.5 fusion.3
  419.6 38.8 %all-to-all-done.4 = bf16[128,128,128]{2,1,0:T(8,128)(2,1)} async-done(((bf16[128,128,128]{2,1,0:T(8,128)(2,1)}), bf16[128,128,128]{2,1,0:T(8,128)(2,1)}, u32[]{:S(2)}, u32[]{:S(2)}) %all-to-all-start.4) | async-done | bytes 4194336 | tf_op jit(solution)/shard_map/all_to_all | solution.py:148
  458.3 23.9 %shard_map.81 = f32[4,512,128]{2,1,0:T(8,128)} custom-call(bf16[32,16,8,128]{3,2,1,0:T(8,128)(2,1)} %bitcast.81, bf16[32,4,128,128]{3,2,1,0:T(8,128)(2,1)} %bitcast.20.grad_ref), custom_call_target="tpu_custom_call" | custom-call | flops 5368709120 | bytes 4194304 | tf_op jit(solution)/shard_map/pallas_call | solution.py:99
  483.8 2.4 fusion.2
  486.3 7.5 %all-gather = f32[4,16,512]{2,0,1:T(4,128)S(1)} all-gather(f32[4,4,512]{2,0,1:T(4,128)S(1)} %copy.24), channel_id=2, replica_groups=mesh['group'=4,'shard'=8] {'group'}, dimensions={1}, use_global_device_ids=true | all-gather | bytes 163840 | tf_op jit(solution)/shard_map/all_gather | solution.py:165
  494.5 24.4 %all-gather.12.cloned.1.call-done = bf16[16,512,128]{2,1,0:T(8,128)(2,1)} async-done(((bf16[4,512,128]{2,1,0:T(8,128)(2,1)}), bf16[16,512,128]{2,1,0:T(8,128)(2,1)}) %all-gather.12.cloned.1.call-update) | async-done | bytes 2097168 | tf_op jit(solution)/shard_map/all_gather | solution.py:162
  519.0 7.2 %pad_maximum_fusion = bf16[64,512,128]{2,1,0:T(8,128)(2,1)} fusion(bf16[16,512,128]{2,1,0:T(8,128)(2,1)} %all-gather.12.cloned.1.call-done, bf16[16,512,128]{2,1,0:T(8,128)(2,1)} %all-gather.10.cloned.1.call-done, bf16[16,512,128]{2,1,0:T(8,128)(2,1)} %all-gather.8.cloned.1.call-done, bf16[16,512,128]{2,1,0:T(8,128)(2,1)} %all-gather.6.cloned.1.call-done), kind=kLoop, calls=%fused_computation.1 | loop fusion | flops 12582912 | bytes 16777216 | tf_op jit(solution)/shard_map/concatenate | solution.py:167
  (43 shorter events, 10.6 us)
Async XLA Ops:
  131.4 98.5 %all-to-all-start.2 = ((bf16[128,128,128]{2,1,0:T(8,128)(2,1)}), bf16[128,128,128]{2,1,0:T(8,128)(2,1)}, u32[]{:S(2)}, u32[]{:S(2)}) async-start(bf16[128,128,128]{2,1,0:T(8,128)(2,1)} %get-tuple-element.16), calls=%async_computation.2 | async-start | bytes 8388608 | tf_op jit(solution)/shard_map/all_to_all | solution.py:148
  135.2 2.4 copy-start.1
  230.0 30.1 %all-to-all-start = ((bf16[512,8,128]{2,1,0:T(8,128)(2,1)}), bf16[512,8,128]{2,1,0:T(8,128)(2,1)S(1)}, u32[]{:S(2)}, u32[]{:S(2)}) async-start(bf16[512,8,128]{2,1,0:T(8,128)(2,1)} %gather_fusion), calls=%async_computation | async-start | bytes 2097152 | tf_op jit(solution)/shard_map/all_to_all | solution.py:139
  232.6 32.2 %copy-start.2 = (f32[64,512]{1,0:T(8,128)S(1)}, f32[64,512]{1,0:T(8,128)}, u32[]{:S(2)}) copy-start(f32[64,512]{1,0:T(8,128)} %param.11) | copy-start | bytes 393220
  260.1 1.1 copy-start
  261.2 98.5 %all-to-all-start.3 = ((bf16[128,128,128]{2,1,0:T(8,128)(2,1)}), bf16[128,128,128]{2,1,0:T(8,128)(2,1)}, u32[]{:S(2)}, u32[]{:S(2)}) async-start(bf16[128,128,128]{2,1,0:T(8,128)(2,1)} %get-tuple-element.19), calls=%async_computation.3 | async-start | bytes 8388608 | tf_op jit(solution)/shard_map/all_to_all | solution.py:148
  264.7 229.8 %all-gather.6.cloned.1.call-start = ((), (), s32[]{:S(2)}) async-start(), calls=%async_computation.5 | async-start | bytes 2621440 | tf_op jit(solution)/shard_map/all_gather | solution.py:162
  359.7 98.6 %all-to-all-start.4 = ((bf16[128,128,128]{2,1,0:T(8,128)(2,1)}), bf16[128,128,128]{2,1,0:T(8,128)(2,1)}, u32[]{:S(2)}, u32[]{:S(2)}) async-start(bf16[128,128,128]{2,1,0:T(8,128)(2,1)} %get-tuple-element.21), calls=%async_computation.4 | async-start | bytes 8388608 | tf_op jit(solution)/shard_map/all_to_all | solution.py:148
  363.3 131.3 %all-gather.8.cloned.1.call-start = ((), (), s32[]{:S(2)}) async-start(), calls=%async_computation.6 | async-start | bytes 2621440 | tf_op jit(solution)/shard_map/all_gather | solution.py:162
  391.4 103.2 %all-gather.10.cloned.1.call-start = ((), (), s32[]{:S(2)}) async-start(), calls=%async_computation.7 | async-start | bytes 2621440 | tf_op jit(solution)/shard_map/all_gather | solution.py:162
  419.5 99.5 %all-gather.12.cloned.1.call-start = ((), (), s32[]{:S(2)}) async-start(), calls=%async_computation.8 | async-start | bytes 2621440 | tf_op jit(solution)/shard_map/all_gather | solution.py:162
Sparse Core Ops, SparseCore 0:
  298.8 43.7 all-gather.5
  391.5 48.1 all-gather.7
  441.5 35.5 all-gather.9
  486.4 32.5 all-gather.11
